TPU v7x, 32 devices: a whole 2x2x4 slice. The times are simulated.
32 devices in a mesh: grp: 2 (over x), path: 8 (over z, y), amp: 2 (over core).
Axes of the slice: x: 2, y: 2, z: 4, core: 2. Of those that a mesh axis runs over, the one named last changes fastest.
Arguments:
- left_slabs: bfloat16 [256, 2, 16384], P(('grp', 'path'), None, 'amp'), parts along dimension 0, may hold values from -0.59765625 to 0.59765625
- right_slabs: bfloat16 [256, 2, 8192], P(('grp', 'path'), None, 'amp'), parts along dimension 0, may hold values from -0.59765625 to 0.59765625
- term_index: int32 [256], P(('grp', 'path')), parts along dimension 0, may hold values from 0 to 3
- left_terms: float32 [4, 2, 2, 2], replicated, may hold values from -4.2 to 4.2
- right_terms: float32 [4, 2, 2, 2], replicated, may hold values from -4.2 to 4.2
- left_gates: bfloat16 [2, 2, 128, 128], replicated, may hold values from -0.375 to 0.375
- right_gates: bfloat16 [2, 2, 128, 128], replicated, may hold values from -0.375 to 0.375
Outputs:
- amplitudes: bfloat16 [2, 32768, 8192], P(None, ('grp', 'path'), 'amp'), parts along dimension 1
There are 2 independent parts, one for each index of `grp`. A program takes and returns all parts, laid end to end along the dimension named above; an argument that names none is the same for every part. Nothing has to cross between parts.
All inputs are finite; a program needn't handle non-finite values.
Results may differ from a plain program's by a relative error of at most 0.0081.
Values may be sent and summed in bfloat16 or wider, within the bound.
No kernel may reach another device: no remote copies, remote signals or barrier semaphores. Data moves between devices by JAX's collectives and lax.ppermute only.
A program may use at most 128 MiB of HBM per device.

v0:
```python
import jax
import jax.numpy as jnp
from jax import lax
from jax.sharding import PartitionSpec as P


def cut_term(slab, term_mix):
    paths_here, _, length = slab.shape
    width = min(128, length)
    values = slab.astype(jnp.float32).reshape(paths_here, 2, length // width, width)
    identity = jnp.eye(width // 2, dtype=jnp.float32)

    def expand(part):
        return jnp.einsum("ab,nmj->najbm", identity, part).reshape(paths_here, width, width)

    real_kron = expand(term_mix[:, 0])
    imag_kron = expand(term_mix[:, 1])
    batch_dims = (((2,), (1,)), ((0,), (0,)))

    def times(rows, kron):
        return lax.dot_general(
            rows,
            kron,
            batch_dims,
            precision=lax.Precision.HIGHEST,
            preferred_element_type=jnp.float32,
        )

    real_rows = values[:, 0]
    imag_rows = values[:, 1]
    real_part = times(real_rows, real_kron) - times(imag_rows, imag_kron)
    imag_part = times(real_rows, imag_kron) + times(imag_rows, real_kron)
    return jnp.stack([real_part, imag_part], 1).reshape(paths_here, 2, length).astype(jnp.bfloat16)


def apply_low(slab, gate_mat):
    paths_here, _, length = slab.shape
    gate_width = gate_mat.shape[-1]
    real_rows = slab[:, 0].reshape(-1, gate_width)
    imag_rows = slab[:, 1].reshape(-1, gate_width)
    upper = jnp.concatenate([gate_mat[0].T, gate_mat[1].T], 1)
    lower = jnp.concatenate([-gate_mat[1].T, gate_mat[0].T], 1)
    right_matrix = jnp.concatenate([upper, lower], 0)
    product = jnp.dot(
        jnp.concatenate([real_rows, imag_rows], 1), right_matrix, preferred_element_type=jnp.float32
    )
    real_part = product[:, :gate_width].reshape(paths_here, length)
    imag_part = product[:, gate_width:].reshape(paths_here, length)
    return jnp.stack([real_part, imag_part], 1).astype(jnp.bfloat16)


def stack_matrix(gate_mat):
    upper = jnp.concatenate([gate_mat[0], -gate_mat[1]], 1)
    lower = jnp.concatenate([gate_mat[1], gate_mat[0]], 1)
    return jnp.concatenate([upper, lower], 0)


def gate_rows(matrix, data):
    batch = jnp.broadcast_to(matrix, (data.shape[0],) + matrix.shape)
    return lax.dot_general(
        batch, data, (((2,), (1,)), ((0,), (0,))), preferred_element_type=jnp.float32
    )


def right_high(moved, gate_mat):
    half_paths = moved.shape[0]
    gate_width = gate_mat.shape[-1]
    low_width = gate_width // 2
    data = moved.reshape(half_paths, gate_width, gate_width)
    blocks = gate_mat.reshape(2, low_width, 2, low_width, 2)
    rows_index = jnp.arange(gate_width, dtype=jnp.int32)[:, None]
    cols_index = jnp.arange(gate_width, dtype=jnp.int32)[None, :]
    same_slot = rows_index % low_width == cols_index % low_width
    total = jnp.zeros((half_paths, gate_width, gate_width), jnp.float32)
    for target in range(2):
        for source in range(2):
            select = (
                same_slot
                & (rows_index // low_width == source)
                & (cols_index // low_width == target)
            ).astype(jnp.bfloat16)
            placed = jnp.dot(
                data.reshape(-1, gate_width), select, preferred_element_type=jnp.float32
            )
            placed = placed.astype(jnp.bfloat16).reshape(half_paths, gate_width, gate_width)
            matrix = stack_matrix(blocks[:, :, target, :, source])
            total = total + gate_rows(matrix, placed)
    return total.astype(jnp.bfloat16).reshape(half_paths, 2, -1)


def contract(left_part, right_part):
    left_stack = jnp.concatenate([left_part[:, 0], left_part[:, 1]], 0)
    right_real = jnp.concatenate([right_part[:, 0], -right_part[:, 1]], 0)
    right_imag = jnp.concatenate([right_part[:, 1], right_part[:, 0]], 0)
    contract_dims = (((0,), (0,)), ((), ()))
    real_part = lax.dot_general(
        left_stack, right_real, contract_dims, preferred_element_type=jnp.float32
    )
    imag_part = lax.dot_general(
        left_stack, right_imag, contract_dims, preferred_element_type=jnp.float32
    )
    return (real_part, imag_part)


def mixes(term_index, terms):
    chosen = (term_index[:, None] == jnp.arange(terms.shape[0], dtype=jnp.int32)[None, :]).astype(
        jnp.float32
    )
    flat = jnp.dot(chosen, terms.reshape(terms.shape[0], 8), precision=lax.Precision.HIGHEST)
    return flat.reshape(-1, 2, 2, 2)


def shards(left_slabs, right_slabs, term_index, left_terms, right_terms, left_gates, right_gates):
    gate_width = left_gates.shape[-1]
    path_count = lax.axis_size("path")
    left = cut_term(left_slabs, mixes(term_index, left_terms))
    left = apply_low(left, left_gates[0])
    moved = lax.all_to_all(left, "amp", split_axis=0, concat_axis=2, tiled=True)
    half_paths = moved.shape[0]
    full_left = moved.shape[2]
    turned = gate_rows(
        stack_matrix(left_gates[1]),
        moved.reshape(half_paths, 2 * gate_width, full_left // gate_width),
    )
    turned = turned.astype(jnp.bfloat16).reshape(half_paths, 2, full_left)
    portion = lax.all_to_all(turned, "path", split_axis=2, concat_axis=0, tiled=True)
    rows_here = portion.shape[2]
    portion = portion.reshape(path_count, half_paths, 2, rows_here)
    row_block = lax.all_gather(portion, "amp", axis=1, tiled=True).reshape(
        path_count * half_paths * 2, 2, rows_here
    )
    right = cut_term(right_slabs, mixes(term_index, right_terms))
    right = apply_low(right, right_gates[0])
    right_moved = lax.all_to_all(right, "amp", split_axis=0, concat_axis=2, tiled=True)
    right_turned = right_high(right_moved, right_gates[1])
    right = lax.all_to_all(right_turned, "amp", split_axis=2, concat_axis=0, tiled=True)
    everything = lax.all_gather(right, "path", axis=0, tiled=True)
    real_part, imag_part = contract(row_block, everything)
    return jnp.stack([real_part, imag_part], 0).astype(jnp.bfloat16)


def solution(mesh):
    return jax.shard_map(
        shards,
        mesh=mesh,
        in_specs=(
            P(("grp", "path"), None, "amp"),
            P(("grp", "path"), None, "amp"),
            P(("grp", "path")),
            P(),
            P(),
            P(),
            P(),
        ),
        out_specs=P(None, ("grp", "path"), "amp"),
        check_vma=False,
    )
```

profile of v0, /device:TPU:0, one launch (start us, length us, event | category | flops | bytes accessed | tf_op | source)
XLA Modules:
  0.0 288.8 jit_solution(7753225383539384605)
XLA Ops:
  6.5 0.8 fusion.80
  7.3 0.8 slice_bitcast_fusion.20
  8.1 0.8 fusion.68
  9.0 0.8 fusion.66
  9.8 1.4 reshape.234
  11.3 18.8 %broadcast_multiply_fusion.3 = (f32[16,2,2,64,64]{0,1,4,2,3:T(2,128)}, f32[16,2,2,64,64]{0,1,4,2,3:T(2,128)}, f32[16,2,2,64,64]{0,1,4,2,3:T(2,128)}, f32[16,2,2,64,64]{0,1,4,2,3:T(2,128)}) fusion(f32[64,64]{1,0:T(8,128)S(1)} %fusion.61, f32[16,2,2]{0,1,2:T(2,128)S(1)} %copy.56, f32[16,2,2]{0,1,2:T(2,128)S(1)} %copy.59, f32[16,2,2]{0,1,2:T(2,128)S(1)} %copy.69, ...), kind=kLoop, calls=%fused_computation.6 | loop fusion | flops 1048576 | bytes 4211712 | tf_op jit(solution)/shard_map/ab,nmj->najbm/dot_general | solution.py:14
  30.1 5.2 %copy.58 = f32[16,128,128]{2,1,0:T(8,128)S(1)} copy(f32[16,128,128]{0,2,1:T(8,128)} %bitcast.165) | data formatting | bytes 2097152 | tf_op jit(solution)/shard_map/reshape | solution.py:14
  35.3 5.2 %copy.60 = f32[16,128,128]{2,1,0:T(8,128)S(1)} copy(f32[16,128,128]{0,2,1:T(8,128)} %bitcast.164) | data formatting | bytes 2097152 | tf_op jit(solution)/shard_map/reshape | solution.py:14
  40.6 0.6 fusion.18
  41.2 0.6 fusion.19
  41.9 0.6 fusion.7
  42.5 0.6 fusion.6
  43.1 0.3 convolution_convert_fusion
  43.5 0.1 stack_reshape.20
  43.7 0.1 stack_reshape.21
  43.8 2.0 pad_maximum_fusion.4
  45.8 3.7 %all-to-all-start = ((bf16[16,2,8192]{2,1,0:T(2,128)(2,1)}), bf16[16,2,8192]{2,1,0:T(2,128)(2,1)S(1)}, u32[]{:S(2)}, u32[]{:S(2)}) async-start(bf16[16,2,8192]{2,1,0:T(2,128)(2,1)} %pad_maximum_fusion.4), calls=%async_computation | async-start | bytes 1048576 | tf_op jit(solution)/shard_map/all_to_all | solution.py:118
  49.5 0.8 fusion.79
  50.3 0.2 reshape.235
  50.5 10.0 %reshape_squeeze.17 = bf16[2,64,2,64,2]{4,3,2,1,0:T(8,128)(2,1)} reshape(bf16[1,2,128,128]{3,2,1,0:T(8,128)(2,1)S(1)} %slice-done) | data formatting | bytes 131072 | tf_op jit(solution)/shard_map/reshape;squeeze | solution.py:70
  60.5 7.9 %slice_reduce_fusion = (bf16[64,64]{1,0:T(8,128)(2,1)S(1)}, bf16[64,64]{1,0:T(8,128)(2,1)S(1)}, bf16[64,64]{1,0:T(8,128)(2,1)S(1)}, bf16[64,64]{1,0:T(8,128)(2,1...) fusion(bf16[2,64,2,64,2]{4,3,2,1,0:T(8,128)(2,1)} %reshape_sque, ...), kind=kLoop, calls=%fused_computation.34 | loop fusion | bytes 131072 | tf_op jit(solution)/shard_map/slice | solution.py:53
  68.5 5.2 %copy.71 = f32[16,128,128]{2,1,0:T(8,128)S(1)} copy(f32[16,128,128]{0,2,1:T(8,128)} %bitcast.163) | data formatting | bytes 2097152 | tf_op jit(solution)/shard_map/reshape | solution.py:14
  73.8 5.2 %copy.73 = f32[16,128,128]{2,1,0:T(8,128)S(1)} copy(f32[16,128,128]{0,2,1:T(8,128)} %bitcast.162) | data formatting | bytes 2097152 | tf_op jit(solution)/shard_map/reshape | solution.py:14
  79.0 0.6 fusion.40
  79.6 0.6 fusion.39
  80.2 0.6 fusion.9
  80.9 0.6 fusion.10
  81.5 0.3 convolution_convert_fusion.6
  81.9 1.3 pad_maximum_fusion.5
  83.2 3.4 %all-to-all-start.2 = ((bf16[16,2,4096]{2,1,0:T(2,128)(2,1)}), bf16[16,2,4096]{2,1,0:T(2,128)(2,1)S(1)}, u32[]{:S(2)}, u32[]{:S(2)}) async-start(bf16[16,2,4096]{2,1,0:T(2,128)(2,1)} %pad_maximum_fusion.5), calls=%async_computation.2 | async-start | bytes 524288 | tf_op jit(solution)/shard_map/all_to_all | solution.py:134
  86.6 0.5 copy.95
  87.2 0.4 reshape.221
  87.6 0.4 convolution_convert_fusion.1
  88.0 0.1 reshape.222
  88.2 12.8 %copy.66 = bf16[8,2,16384]{0,1,2:T(2,128)(2,1)} copy(bf16[8,2,16384]{2,1,0:T(2,128)(2,1)S(1)} %reshape.222) | data formatting | bytes 1048576 | tf_op jit(solution)/shard_map/reshape | solution.py:125
  100.9 11.1 %reshape.246 = bf16[8,2,16384]{2,1,0:T(2,128)(2,1)} reshape(bf16[16384,2,8]{2,1,0:T(2,128)(2,1)} %bitcast.160) | data formatting | bytes 1048576
  112.1 7.3 %all-to-all-start.1 = ((bf16[8,2,16384]{2,1,0:T(2,128)(2,1)}), bf16[8,2,16384]{2,1,0:T(2,128)(2,1)S(1)}, u32[]{:S(2)}, u32[]{:S(2)}) async-start(bf16[8,2,16384]{2,1,0:T(2,128)(2,1)} %reshape.246), calls=%async_computation.1 | async-start | bytes 1048576 | tf_op jit(solution)/shard_map/all_to_all | solution.py:126
  119.4 0.3 all-gather.3.cloned.1.call-start
  119.7 0.2 copy.96
  119.8 0.3 copy.79
  120.1 0.2 reshape_reshape.2
  120.4 0.3 convolution_convert_fusion.2
  120.7 0.3 convolution_convert_fusion.3
  121.0 0.3 convolution_convert_fusion.4
  121.3 0.3 convolution_convert_fusion.5
  121.6 12.9 %all-to-all-done.1 = bf16[8,2,16384]{2,1,0:T(2,128)(2,1)S(1)} async-done(((bf16[8,2,16384]{2,1,0:T(2,128)(2,1)}), bf16[8,2,16384]{2,1,0:T(2,128)(2,1)S(1)}, u32[]{:S(2)}, u32[]{:S(2)}) %all-to-all-start.1) | async-done | bytes 524320 | tf_op jit(solution)/shard_map/all_to_all | solution.py:126
  134.5 10.9 %reshape.247 = bf16[16384,2,8]{2,1,0:T(2,128)(2,1)} reshape(bf16[8,2,16384]{2,1,0:T(2,128)(2,1)S(1)} %all-to-all-done.1) | data formatting | bytes 1048576
  145.4 12.5 %copy.85 = bf16[8,2,8,2048]{3,2,0,1:T(8,128)(2,1)} copy(bf16[8,2,8,2048]{0,1,3,2:T(2,128)(2,1)} %bitcast.161) | data formatting | bytes 1048576 | tf_op jit(solution)/shard_map/all_to_all | solution.py:126
  158.1 0.2 fusion.37
  158.3 0.2 convolution_add_fusion.3
  158.6 0.2 convolution_add_fusion.2
  158.8 0.2 fusion.8
  159.1 6.8 %copy.80 = bf16[8,2,8192]{0,1,2:T(2,128)(2,1)} copy(bf16[8,2,8192]{2,1,0:T(2,128)(2,1)S(1)} %reshape.232) | data formatting | bytes 524288 | tf_op jit(solution)/shard_map/reshape | solution.py:88
  165.9 6.1 %reshape.244 = bf16[2,2,32768]{2,1,0:T(2,128)(2,1)S(1)} reshape(bf16[8192,2,8]{2,1,0:T(2,128)(2,1)} %bitcast.166) | data formatting | bytes 524288
  172.0 3.9 %all_to_all.63 = bf16[2,2,32768]{2,1,0:T(2,128)(2,1)S(1)} all-to-all(bf16[2,2,32768]{2,1,0:T(2,128)(2,1)S(1)} %reshape.244), channel_id=1, replica_groups=mesh['grp'=2,'path'=8,'amp'=2] {'amp'}, dimensions={0} | all-to-all | bytes 524288 | tf_op jit(solution)/shard_map/all_to_all | solution.py:136
  175.9 6.2 %reshape.245 = bf16[8192,2,8]{2,1,0:T(2,128)(2,1)} reshape(bf16[2,2,32768]{2,1,0:T(2,128)(2,1)S(1)} %all_to_all.63) | data formatting | bytes 524288
  182.1 9.3 %copy.82 = bf16[2,8,2,4096]{3,1,0,2:T(8,128)(2,1)} copy(bf16[2,8,2,4096]{1,2,3,0:T(2,128)(2,1)} %bitcast.167) | data formatting | bytes 524288 | tf_op jit(solution)/shard_map/all_to_all | solution.py:136
  191.4 1.8 copy.68
  193.4 46.4 %all-gather.5.cloned.1.call-done = bf16[128,2,4096]{2,0,1:T(8,128)(2,1)} async-done(((bf16[16,2,4096]{2,0,1:T(8,128)(2,1)}), bf16[128,2,4096]{2,0,1:T(8,128)(2,1)}) %all-gather.5.cloned.1.call-update) | async-done | bytes 2097168 | tf_op jit(solution)/shard_map/all_gather | solution.py:137
  239.8 1.7 slice_bitcast_fusion
  241.5 8.1 %convert_bitcast_fusion = bf16[1,2048,4096]{2,1,0:T(8,128)(2,1)} fusion(bf16[128,4096]{1,0:T(8,128)(2,1)S(1)} %get-tuple-element.14, bf16[128,4096]{1,0:T(8,128)(2,1)S(1)} %get-tuple-element.13, bf16[128,2048]{1,0:T(8,128)(2,1)S(1)} %get-tuple-element.16, bf16[128,2048]{1,0:T(8,128)(2,1)S(1)} %get-tuple-element.15), kind=kOutput, calls=%fused_computation.1 | convolution fusion | flops 4309647360 | bytes 19922944 | tf_op jit(solution)/shard_map/dot_general | solution.py:99
  249.6 1.3 fusion.82
  250.9 8.1 %convert_bitcast_fusion.1 = bf16[1,2048,4096]{2,1,0:T(8,128)(2,1)} fusion(bf16[128,4096]{1,0:T(8,128)(2,1)S(1)} %fusion.82, bf16[128,4096]{1,0:T(8,128)(2,1)S(1)} %get-tuple-element.14, bf16[128,2048]{1,0:T(8,128)(2,1)S(1)} %get-tuple-element.16, bf16[128,2048]{1,0:T(8,128)(2,1)S(1)} %get-tuple-element.15), kind=kOutput, calls=%fused_computation.2 | convolution fusion | flops 4309647360 | bytes 19922944 | tf_op jit(solution)/shard_map/dot_general | solution.py:96
  259.0 23.0 %pad_maximum_fusion = bf16[2,2048,4096]{2,1,0:T(8,128)(2,1)} fusion(bf16[1,2048,4096]{2,1,0:T(8,128)(2,1)} %convert_bitcast_fusion, bf16[1,2048,4096]{2,1,0:T(8,128)(2,1)} %convert_bitcast_fusion.1), kind=kLoop, calls=%fused_computation | loop fusion | flops 16777216 | bytes 67108864 | tf_op jit(solution)/shard_map/stack | solution.py:139
  (40 shorter events, 0.7 us)
Async XLA Ops:
  6.5 1.6 copy-start
  40.6 9.7 %copy-start.2 = (bf16[2,2,128,128]{3,2,1,0:T(8,128)(2,1)S(1)}, bf16[2,2,128,128]{3,2,1,0:T(8,128)(2,1)}, u32[]{:S(2)}) copy-start(bf16[2,2,128,128]{3,2,1,0:T(8,128)(2,1)} %param.13) | copy-start | bytes 393220
  40.6 9.7 %copy-start.3 = (bf16[16,2,4096]{2,1,0:T(2,128)(2,1)S(1)}, bf16[16,2,4096]{2,1,0:T(2,128)(2,1)}, u32[]{:S(2)}) copy-start(bf16[16,2,4096]{2,1,0:T(2,128)(2,1)} %param.8) | copy-start | bytes 786436
  40.6 9.9 %slice-start = ((bf16[2,2,128,128]{3,2,1,0:T(8,128)(2,1)}), bf16[1,2,128,128]{3,2,1,0:T(8,128)(2,1)S(1)}, s32[]{:S(2)}) async-start(bf16[2,2,128,128]{3,2,1,0:T(8,128)(2,1)} %param.13), calls=%async_computation.6 | async-start | bytes 131072 | tf_op jit(solution)/shard_map/slice | solution.py:135
  45.8 37.4 %all-to-all-start = ((bf16[16,2,8192]{2,1,0:T(2,128)(2,1)}), bf16[16,2,8192]{2,1,0:T(2,128)(2,1)S(1)}, u32[]{:S(2)}, u32[]{:S(2)}) async-start(bf16[16,2,8192]{2,1,0:T(2,128)(2,1)} %pad_maximum_fusion.4), calls=%async_computation | async-start | bytes 1048576 | tf_op jit(solution)/shard_map/all_to_all | solution.py:118
  83.2 28.9 %all-to-all-start.2 = ((bf16[16,2,4096]{2,1,0:T(2,128)(2,1)}), bf16[16,2,4096]{2,1,0:T(2,128)(2,1)S(1)}, u32[]{:S(2)}, u32[]{:S(2)}) async-start(bf16[16,2,4096]{2,1,0:T(2,128)(2,1)} %pad_maximum_fusion.5), calls=%async_computation.2 | async-start | bytes 524288 | tf_op jit(solution)/shard_map/all_to_all | solution.py:134
  112.1 22.5 %all-to-all-start.1 = ((bf16[8,2,16384]{2,1,0:T(2,128)(2,1)}), bf16[8,2,16384]{2,1,0:T(2,128)(2,1)S(1)}, u32[]{:S(2)}, u32[]{:S(2)}) async-start(bf16[8,2,16384]{2,1,0:T(2,128)(2,1)} %reshape.246), calls=%async_computation.1 | async-start | bytes 1048576 | tf_op jit(solution)/shard_map/all_to_all | solution.py:126
  119.4 72.0 %all-gather.3.cloned.1.call-start = ((), (), s32[]{:S(2)}) async-start(), calls=%async_computation.4 | async-start | bytes 1572864 | tf_op jit(solution)/shard_map/all_gather | solution.py:129
  158.0 81.8 %all-gather.5.cloned.1.call-start = ((), (), s32[]{:S(2)}) async-start(), calls=%async_computation.5 | async-start | bytes 2359296 | tf_op jit(solution)/shard_map/all_gather | solution.py:137
  259.0 23.0 %copy-start.1 = (f32[4,2,2,2]{0,3,2,1:T(2,128)S(1)}, f32[4,2,2,2]{0,3,2,1:T(2,128)}, u32[]{:S(2)}) copy-start(f32[4,2,2,2]{0,3,2,1:T(2,128)} %param.10) | copy-start | bytes 388
Sparse Core Ops, SparseCore 0:
  158.1 8.0 all-gather.2
  191.5 48.2 all-gather.4
where the time goes:
time: 290 us; the launch traced here: 289 us
  local copies, waits for them, and re-layouts  123 us (42%)
  waiting for transfers between devices  59.4 us (20%)
  other arithmetic  48.2 us (17%)
  matrix products  25.9 us (9%)
  starting transfers between devices  14.7 us (5%)
  between operations  13.9 us (5%)
  blocking collectives  3.94 us (1%)
    all_gather x1, waiting for transfers between devices, shards(): everything = lax.all_gather(right, 'path', axis=0, tiled=True)  46.4 us
    unnamed x12, local copies, waits for them, and re-layouts  34.3 us
    another operation x1, other arithmetic, shards(): return jnp.stack([real_part, imag_part], 0).astype(jnp.bfloat16)  23 us
    reshape x4, local copies, waits for them, and re-layouts, expand(): jnp.einsum('ab,nmj->najbm', identity, part)  20.9 us
    dot_general x1, other arithmetic, expand(): jnp.einsum('ab,nmj->najbm', identity, part)  18.8 us
    reshape x2, local copies, waits for them, and re-layouts, shards(): turned = turned.astype(jnp.bfloat16).reshape(half_paths, 2, full_left)  12.9 us
    all_to_all x1, waiting for transfers between devices, shards(): lax.all_to_all(turned, 'path', split_axis=2, concat_axis=0, tiled=True)  12.9 us
    all_to_all x1, local copies, waits for them, and re-layouts, shards(): lax.all_to_all(turned, 'path', split_axis=2, concat_axis=0, tiled=True)  12.5 us
  transfers between devices with their start and end apart: 5, of which 2 were waited for; matrix products, arithmetic and copies ran while one was open for 32% of the time, Pallas kernels for 0%

commit v1 on v0

--- a/solution.py
+++ b/solution.py
@@ -134,7 +134,14 @@
     right_moved = lax.all_to_all(right, "amp", split_axis=0, concat_axis=2, tiled=True)
     right_turned = right_high(right_moved, right_gates[1])
     right = lax.all_to_all(right_turned, "amp", split_axis=2, concat_axis=0, tiled=True)
-    everything = lax.all_gather(right, "path", axis=0, tiled=True)
+    size = lax.axis_size("path")
+    route = [(i, (i + 1) % size) for i in range(size)]
+    terms_2 = [right]
+    for far in range(1, size):
+        terms_2 = [lax.ppermute(terms_2[0], "path", route), *terms_2]
+    whole = jnp.concatenate(terms_2, axis=0)
+    shift = (lax.axis_index("path") + 1) * terms_2[-1].shape[0]
+    everything = jnp.roll(whole, shift, axis=0)
     real_part, imag_part = contract(row_block, everything)
     return jnp.stack([real_part, imag_part], 0).astype(jnp.bfloat16)
 

time: 290 us -> 283 us (0.976)
  waiting for transfers between devices: 59.4 us -> 46.5 us
  blocking collectives: 3.94 us -> 8.1 us
    all_gather x1 -> x0, waiting for transfers between devices: 46.4 us -> none  [shards(): everything = lax.all_gather(right, 'path', axis=0, tiled=True)]
    ppermute x0 -> x7, waiting for transfers between devices: none -> 36.2 us  [shards(): terms_2 = [lax.ppermute(terms_2[0], 'path', route), *terms_2]]
    all_to_all x1, waiting for transfers between devices: 12.9 us -> 0.01 us  [shards(): lax.all_to_all(turned, 'path', split_axis=2, concat_axis=0, tiled=True)]
    all_gather x1, waiting for transfers between devices: 0.02 us -> 8.84 us  [shards(): lax.all_gather(portion, 'amp', axis=1, tiled=True)]
    ppermute x0 -> x7, starting transfers between devices: none -> 6.71 us  [shards(): terms_2 = [lax.ppermute(terms_2[0], 'path', route), *terms_2]]
    all_to_all x0 -> x1, blocking collectives: none -> 4.15 us  [shards(): moved = lax.all_to_all(left, 'amp', split_axis=0, concat_axis=2, tiled=True)]
    all_to_all x1 -> x0, starting transfers between devices: 3.67 us -> none  [shards(): moved = lax.all_to_all(left, 'amp', split_axis=0, concat_axis=2, tiled=True)]
    unnamed x12 -> x33, local copies, waits for them, and re-layouts: 34.3 us -> 34.6 us
  transfers between devices with their start and end apart: 5 -> 10, of which waited for: 2 -> 6; matrix products, arithmetic and copies ran while one was open for 32% -> 24% of each run, Pallas kernels for 0% -> 0%
where the time goes in v1:
time: 283 us; the launch traced here: 281 us
  local copies, waits for them, and re-layouts  121 us (43%)
  other arithmetic  48 us (17%)
  waiting for transfers between devices  46.5 us (16%)
  matrix products  27.2 us (10%)
  starting transfers between devices  16.4 us (6%)
  between operations  14 us (5%)
  blocking collectives  8.1 us (3%)
    ppermute x7, waiting for transfers between devices, shards(): terms_2 = [lax.ppermute(terms_2[0], 'path', route), *terms_2]  36.2 us
    unnamed x33, local copies, waits for them, and re-layouts  34.6 us
    another operation x1, other arithmetic, shards(): return jnp.stack([real_part, imag_part], 0).astype(jnp.bfloat16)  23 us
    reshape x4, local copies, waits for them, and re-layouts, expand(): jnp.einsum('ab,nmj->najbm', identity, part)  20.9 us
    dot_general x1, other arithmetic, expand(): jnp.einsum('ab,nmj->najbm', identity, part)  18.9 us
    reshape x2, local copies, waits for them, and re-layouts, shards(): turned = turned.astype(jnp.bfloat16).reshape(half_paths, 2, full_left)  12.9 us
    all_to_all x1, local copies, waits for them, and re-layouts, shards(): lax.all_to_all(turned, 'path', split_axis=2, concat_axis=0, tiled=True)  12.5 us
    another operation x1, local copies, waits for them, and re-layouts, right_high(): blocks = gate_mat.reshape(2, low_width, 2, low_width, 2)  10 us
  transfers between devices with their start and end apart: 10, of which 6 were waited for; matrix products, arithmetic and copies ran while one was open for 24% of the time, Pallas kernels for 0%

profile of v1, /device:TPU:0, one launch (start us, length us, event | category | flops | bytes accessed | tf_op | source)
XLA Modules:
  0.0 281.5 jit_solution(17611602408648120674)
XLA Ops:
  6.5 0.8 fusion.81
  7.3 0.8 slice_bitcast_fusion.14
  8.1 0.8 fusion.68
  8.9 0.8 fusion.66
  9.8 1.2 reshape.235
  10.9 18.9 %broadcast_multiply_fusion.3 = (f32[16,2,2,64,64]{0,1,4,2,3:T(2,128)}, f32[16,2,2,64,64]{0,1,4,2,3:T(2,128)}, f32[16,2,2,64,64]{0,1,4,2,3:T(2,128)}, f32[16,2,2,64,64]{0,1,4,2,3:T(2,128)}) fusion(f32[64,64]{1,0:T(8,128)S(1)} %fusion.61, f32[16,2,2]{0,1,2:T(2,128)S(1)} %copy.56, f32[16,2,2]{0,1,2:T(2,128)S(1)} %copy.59, f32[16,2,2]{0,1,2:T(2,128)S(1)} %copy.69, ...), kind=kLoop, calls=%fused_computation.6 | loop fusion | flops 1048576 | bytes 4211712 | tf_op jit(solution)/shard_map/ab,nmj->najbm/dot_general | solution.py:14
  29.8 5.2 %copy.71 = f32[16,128,128]{2,1,0:T(8,128)S(1)} copy(f32[16,128,128]{0,2,1:T(8,128)} %bitcast.166) | data formatting | bytes 2097152 | tf_op jit(solution)/shard_map/reshape | solution.py:14
  35.0 5.2 %copy.73 = f32[16,128,128]{2,1,0:T(8,128)S(1)} copy(f32[16,128,128]{0,2,1:T(8,128)} %bitcast.165) | data formatting | bytes 2097152 | tf_op jit(solution)/shard_map/reshape | solution.py:14
  40.3 0.6 fusion.40
  40.9 0.6 fusion.39
  41.5 0.6 fusion.9
  42.1 0.6 fusion.10
  42.7 0.3 convolution_convert_fusion.6
  43.2 1.3 pad_maximum_fusion.5
  44.5 3.6 %all-to-all-start.2 = ((bf16[16,2,4096]{2,1,0:T(2,128)(2,1)}), bf16[16,2,4096]{2,1,0:T(2,128)(2,1)S(1)}, u32[]{:S(2)}, u32[]{:S(2)}) async-start(bf16[16,2,4096]{2,1,0:T(2,128)(2,1)} %pad_maximum_fusion.5), calls=%async_computation.2 | async-start | bytes 524288 | tf_op jit(solution)/shard_map/all_to_all | solution.py:134
  48.1 1.5 all-to-all-done.2
  49.8 0.3 copy.79
  50.3 0.3 convolution_convert_fusion.2
  50.6 0.3 convolution_convert_fusion.3
  50.9 0.3 convolution_convert_fusion.4
  51.2 0.3 convolution_convert_fusion.5
  51.5 10.0 %reshape_squeeze.17 = bf16[2,64,2,64,2]{4,3,2,1,0:T(8,128)(2,1)} reshape(bf16[1,2,128,128]{3,2,1,0:T(8,128)(2,1)S(1)} %slice-done) | data formatting | bytes 131072 | tf_op jit(solution)/shard_map/reshape;squeeze | solution.py:70
  61.6 8.1 %slice_reduce_fusion = (bf16[64,64]{1,0:T(8,128)(2,1)S(1)}, bf16[64,64]{1,0:T(8,128)(2,1)S(1)}, bf16[64,64]{1,0:T(8,128)(2,1)S(1)}, bf16[64,64]{1,0:T(8,128)(2,1...) fusion(bf16[2,64,2,64,2]{4,3,2,1,0:T(8,128)(2,1)} %reshape_sque, ...), kind=kLoop, calls=%fused_computation.34 | loop fusion | bytes 131072 | tf_op jit(solution)/shard_map/slice | solution.py:53
  70.0 0.2 convolution_add_fusion.3
  70.5 0.2 fusion.8
  70.8 6.8 %copy.80 = bf16[8,2,8192]{0,1,2:T(2,128)(2,1)} copy(bf16[8,2,8192]{2,1,0:T(2,128)(2,1)S(1)} %reshape.232) | data formatting | bytes 524288 | tf_op jit(solution)/shard_map/reshape | solution.py:88
  77.7 6.1 %reshape.244 = bf16[2,2,32768]{2,1,0:T(2,128)(2,1)S(1)} reshape(bf16[8192,2,8]{2,1,0:T(2,128)(2,1)} %bitcast.167) | data formatting | bytes 524288
  83.8 3.9 %all_to_all.63 = bf16[2,2,32768]{2,1,0:T(2,128)(2,1)S(1)} all-to-all(bf16[2,2,32768]{2,1,0:T(2,128)(2,1)S(1)} %reshape.244), channel_id=1, replica_groups=mesh['grp'=2,'path'=8,'amp'=2] {'amp'}, dimensions={0} | all-to-all | bytes 524288 | tf_op jit(solution)/shard_map/all_to_all | solution.py:136
  87.7 6.2 %reshape.245 = bf16[8192,2,8]{2,1,0:T(2,128)(2,1)} reshape(bf16[2,2,32768]{2,1,0:T(2,128)(2,1)S(1)} %all_to_all.63) | data formatting | bytes 524288
  93.9 8.2 %copy.82 = bf16[2,8,2,4096]{3,1,0,2:T(8,128)(2,1)S(1)} copy(bf16[2,8,2,4096]{1,2,3,0:T(2,128)(2,1)} %bitcast.168) | data formatting | bytes 524288 | tf_op jit(solution)/shard_map/all_to_all | solution.py:136
  102.1 3.1 %collective-permute-start = (bf16[16,2,4096]{2,0,1:T(8,128)(2,1)S(1)}, bf16[16,2,4096]{2,0,1:T(8,128)(2,1)S(1)}, u32[]{:S(2)}, u32[]{:S(2)}) collective-permute-start(bf16[16,2,4096]{2,0,1:T(8,128)(2,1)S(1)} %bitcast.170), channel_id=1, source_target_pairs={{0,2},{2,4},{4,6},{6,8},{8,10},{10,12},{12,14},{14,0},{1,3},{3,5},... | collective-permute-start | bytes 786440 | tf_op jit(solution)/shard_map/ppermute | solution.py:141
  105.3 0.6 fusion.80
  105.9 0.7 slice_bitcast_fusion.18
  106.5 0.4 reshape.234
  106.9 5.2 %copy.58 = f32[16,128,128]{2,1,0:T(8,128)S(1)} copy(f32[16,128,128]{0,2,1:T(8,128)} %bitcast.164) | data formatting | bytes 2097152 | tf_op jit(solution)/shard_map/reshape | solution.py:14
  112.2 5.2 %copy.60 = f32[16,128,128]{2,1,0:T(8,128)S(1)} copy(f32[16,128,128]{0,2,1:T(8,128)} %bitcast.163) | data formatting | bytes 2097152 | tf_op jit(solution)/shard_map/reshape | solution.py:14
  117.4 0.6 fusion.18
  118.1 0.6 fusion.19
  118.7 0.6 fusion.7
  119.3 0.6 fusion.6
  120.0 0.3 convolution_convert_fusion
  120.7 1.6 collective-permute-start.1
  122.2 1.2 pad_maximum_fusion.4
  123.4 4.2 %all_to_all.64 = bf16[16,2,8192]{2,1,0:T(2,128)(2,1)S(1)} all-to-all(bf16[16,2,8192]{2,1,0:T(2,128)(2,1)S(1)} %pad_maximum_fusion.4), channel_id=1, replica_groups=mesh['grp'=2,'path'=8,'amp'=2] {'amp'}, dimensions={0} | all-to-all | bytes 1048576 | tf_op jit(solution)/shard_map/all_to_all | solution.py:118
  127.6 0.5 copy.95
  128.1 0.4 reshape.221
  128.5 3.0 %collective-permute-done.1 = bf16[16,2,4096]{2,0,1:T(8,128)(2,1)S(1)} collective-permute-done((bf16[16,2,4096]{2,0,1:T(8,128)(2,1)S(1)}, bf16[16,2,4096]{2,0,1:T(8,128)(2,1)S(1)}, u32[]{:S(2)}, u32[]{:S(2)}) %collective-permute-start.1) | collective-permute-done | bytes 262176 | tf_op jit(solution)/shard_map/ppermute | solution.py:141
  131.5 0.9 maximum_maximum_fusion
  132.4 9.0 %collective-permute-done.2 = bf16[16,2,4096]{2,0,1:T(8,128)(2,1)S(1)} collective-permute-done((bf16[16,2,4096]{2,0,1:T(8,128)(2,1)S(1)}, bf16[16,2,4096]{2,0,1:T(8,128)(2,1)S(1)}, u32[]{:S(2)}, u32[]{:S(2)}) %collective-permute-start.2) | collective-permute-done | bytes 262176 | tf_op jit(solution)/shard_map/ppermute | solution.py:141
  141.4 0.4 convolution_convert_fusion.1
  142.0 12.8 %copy.66 = bf16[8,2,16384]{0,1,2:T(2,128)(2,1)} copy(bf16[8,2,16384]{2,1,0:T(2,128)(2,1)S(1)} %reshape.222) | data formatting | bytes 1048576 | tf_op jit(solution)/shard_map/reshape | solution.py:125
  154.8 11.1 %reshape.246 = bf16[8,2,16384]{2,1,0:T(2,128)(2,1)} reshape(bf16[16384,2,8]{2,1,0:T(2,128)(2,1)} %bitcast.161) | data formatting | bytes 1048576
  165.9 6.0 %all-to-all-start.1 = ((bf16[8,2,16384]{2,1,0:T(2,128)(2,1)}), bf16[8,2,16384]{2,1,0:T(2,128)(2,1)S(1)}, u32[]{:S(2)}, u32[]{:S(2)}) async-start(bf16[8,2,16384]{2,1,0:T(2,128)(2,1)} %reshape.246), calls=%async_computation.1 | async-start | bytes 1048576 | tf_op jit(solution)/shard_map/all_to_all | solution.py:126
  171.9 2.0 collective-permute-start.4
  174.0 15.1 %collective-permute-done.4 = bf16[16,2,4096]{2,0,1:T(8,128)(2,1)S(1)} collective-permute-done((bf16[16,2,4096]{2,0,1:T(8,128)(2,1)S(1)}, bf16[16,2,4096]{2,0,1:T(8,128)(2,1)S(1)}, u32[]{:S(2)}, u32[]{:S(2)}) %collective-permute-start.4) | collective-permute-done | bytes 262176 | tf_op jit(solution)/shard_map/ppermute | solution.py:141
  189.1 9.1 %collective-permute-done.5 = bf16[16,2,4096]{2,0,1:T(8,128)(2,1)S(1)} collective-permute-done((bf16[16,2,4096]{2,0,1:T(8,128)(2,1)S(1)}, bf16[16,2,4096]{2,0,1:T(8,128)(2,1)S(1)}, u32[]{:S(2)}, u32[]{:S(2)}) %collective-permute-start.5) | collective-permute-done | bytes 262176 | tf_op jit(solution)/shard_map/ppermute | solution.py:141
  198.1 10.9 %reshape.247 = bf16[16384,2,8]{2,1,0:T(2,128)(2,1)} reshape(bf16[8,2,16384]{2,1,0:T(2,128)(2,1)S(1)} %all-to-all-done.1) | data formatting | bytes 1048576
  209.0 12.5 %copy.85 = bf16[8,2,8,2048]{3,2,0,1:T(8,128)(2,1)} copy(bf16[8,2,8,2048]{0,1,3,2:T(2,128)(2,1)} %bitcast.162) | data formatting | bytes 1048576 | tf_op jit(solution)/shard_map/all_to_all | solution.py:126
  222.1 1.2 fusion.82
  223.3 8.8 %all-gather.2.cloned.1.call-done = bf16[8,16,2,2048]{3,0,1,2:T(8,128)(2,1)} async-done(((bf16[8,8,2,2048]{3,0,1,2:T(8,128)(2,1)}), bf16[8,16,2,2048]{3,0,1,2:T(8,128)(2,1)}) %all-gather.2.cloned.1.call-update) | async-done | bytes 1048592 | tf_op jit(solution)/shard_map/all_gather | solution.py:129
  232.1 1.8 copy.68
  234.1 9.4 %convert_bitcast_fusion = bf16[1,2048,4096]{2,1,0:T(8,128)(2,1)} fusion(bf16[128,4096]{1,0:T(8,128)(2,1)S(1)} %dynamic-slice_bitcast_fusion.1, bf16[128,4096]{1,0:T(8,128)(2,1)} %get-tuple-element.14, bf16[128,2048]{1,0:T(8,128)(2,1)S(1)} %get-tuple-element.16, bf16[128,2048]{1,0:T(8,128)(2,1)S(1)} %get-tuple-element.15), kind=kOutput, calls=%fused_computation.1 | convolution fusion | flops 4309647360 | bytes 19922944 | tf_op jit(solution)/shard_map/dot_general | solution.py:99
  243.4 8.2 %convert_bitcast_fusion.1 = bf16[1,2048,4096]{2,1,0:T(8,128)(2,1)} fusion(bf16[128,4096]{1,0:T(8,128)(2,1)S(1)} %get-tuple-element.13, bf16[128,4096]{1,0:T(8,128)(2,1)S(1)} %dynamic-slice_bitcast_fusion.1, bf16[128,2048]{1,0:T(8,128)(2,1)S(1)} %get-tuple-element.16, bf16[128,2048]{1,0:T(8,128)(2,1)S(1)} %get-tuple-element.15), kind=kOutput, calls=%fused_computation.2 | convolution fusion | flops 4309647360 | bytes 19922944 | tf_op jit(solution)/shard_map/dot_general | solution.py:96
  251.6 23.0 %pad_maximum_fusion = bf16[2,2048,4096]{2,1,0:T(8,128)(2,1)} fusion(bf16[1,2048,4096]{2,1,0:T(8,128)(2,1)} %convert_bitcast_fusion, bf16[1,2048,4096]{2,1,0:T(8,128)(2,1)} %convert_bitcast_fusion.1), kind=kLoop, calls=%fused_computation | loop fusion | flops 16777216 | bytes 67108864 | tf_op jit(solution)/shard_map/stack | solution.py:146
  (72 shorter events, 2.3 us)
Async XLA Ops:
  6.5 1.6 copy-start
  42.1 9.4 %slice-start = ((bf16[2,2,128,128]{3,2,1,0:T(8,128)(2,1)}), bf16[1,2,128,128]{3,2,1,0:T(8,128)(2,1)S(1)}, s32[]{:S(2)}) async-start(bf16[2,2,128,128]{3,2,1,0:T(8,128)(2,1)} %param.13), calls=%async_computation.5 | async-start | bytes 131072 | tf_op jit(solution)/shard_map/slice | solution.py:135
  44.5 5.2 %all-to-all-start.2 = ((bf16[16,2,4096]{2,1,0:T(2,128)(2,1)}), bf16[16,2,4096]{2,1,0:T(2,128)(2,1)S(1)}, u32[]{:S(2)}, u32[]{:S(2)}) async-start(bf16[16,2,4096]{2,1,0:T(2,128)(2,1)} %pad_maximum_fusion.5), calls=%async_computation.2 | async-start | bytes 524288 | tf_op jit(solution)/shard_map/all_to_all | solution.py:134
  87.7 17.5 %copy-start.3 = (bf16[2,2,128,128]{3,2,1,0:T(8,128)(2,1)S(1)}, bf16[2,2,128,128]{3,2,1,0:T(8,128)(2,1)}, u32[]{:S(2)}) copy-start(bf16[2,2,128,128]{3,2,1,0:T(8,128)(2,1)} %param.12) | copy-start | bytes 393220
  87.7 18.8 %copy-start.2 = (bf16[16,2,8192]{2,1,0:T(2,128)(2,1)S(1)}, bf16[16,2,8192]{2,1,0:T(2,128)(2,1)}, u32[]{:S(2)}) copy-start(bf16[16,2,8192]{2,1,0:T(2,128)(2,1)} %param.7) | copy-start | bytes 1572868
  102.1 18.5 %collective-permute-start = (bf16[16,2,4096]{2,0,1:T(8,128)(2,1)S(1)}, bf16[16,2,4096]{2,0,1:T(8,128)(2,1)S(1)}, u32[]{:S(2)}, u32[]{:S(2)}) collective-permute-start(bf16[16,2,4096]{2,0,1:T(8,128)(2,1)S(1)} %bitcast.170), channel_id=1, source_target_pairs={{0,2},{2,4},{4,6},{6,8},{8,10},{10,12},{12,14},{14,0},{1,3},{3,5},... | collective-permute-start | bytes 786440 | tf_op jit(solution)/shard_map/ppermute | solution.py:141
  117.4 2.6 copy-start.4
  117.4 2.6 copy-start.5
  117.4 2.6 copy-start.6
  120.7 10.8 %collective-permute-start.1 = (bf16[16,2,4096]{2,0,1:T(8,128)(2,1)S(1)}, bf16[16,2,4096]{2,0,1:T(8,128)(2,1)S(1)}, u32[]{:S(2)}, u32[]{:S(2)}) collective-permute-start(bf16[16,2,4096]{2,0,1:T(8,128)(2,1)S(1)} %collective-permute-done), channel_id=1, source_target_pairs={{0,2},{2,4},{4,6},{6,8},{8,10},{10,12},{12,14},{14,0},{1,3},{3,5},... | collective-permute-start | bytes 786440 | tf_op jit(solution)/shard_map/ppermute | solution.py:141
  131.5 9.9 %collective-permute-start.2 = (bf16[16,2,4096]{2,0,1:T(8,128)(2,1)S(1)}, bf16[16,2,4096]{2,0,1:T(8,128)(2,1)S(1)}, u32[]{:S(2)}, u32[]{:S(2)}) collective-permute-start(bf16[16,2,4096]{2,0,1:T(8,128)(2,1)S(1)} %collective-permute-done.1), channel_id=1, source_target_pairs={{0,2},{2,4},{4,6},{6,8},{8,10},{10,12},{12,14},{14,0},{1,3},{3,5},... | collective-permute-start | bytes 786440 | tf_op jit(solution)/shard_map/ppermute | solution.py:141
  141.4 30.5 %collective-permute-start.3 = (bf16[16,2,4096]{2,0,1:T(8,128)(2,1)S(1)}, bf16[16,2,4096]{2,0,1:T(8,128)(2,1)S(1)}, u32[]{:S(2)}, u32[]{:S(2)}) collective-permute-start(bf16[16,2,4096]{2,0,1:T(8,128)(2,1)S(1)} %collective-permute-done.2), channel_id=1, source_target_pairs={{0,2},{2,4},{4,6},{6,8},{8,10},{10,12},{12,14},{14,0},{1,3},{3,5},... | collective-permute-start | bytes 786440 | tf_op jit(solution)/shard_map/ppermute | solution.py:141
  165.9 32.2 %all-to-all-start.1 = ((bf16[8,2,16384]{2,1,0:T(2,128)(2,1)}), bf16[8,2,16384]{2,1,0:T(2,128)(2,1)S(1)}, u32[]{:S(2)}, u32[]{:S(2)}) async-start(bf16[8,2,16384]{2,1,0:T(2,128)(2,1)} %reshape.246), calls=%async_computation.1 | async-start | bytes 1048576 | tf_op jit(solution)/shard_map/all_to_all | solution.py:126
  171.9 60.3 %all-gather.2.cloned.1.call-start = ((), (), s32[]{:S(2)}) async-start(), calls=%async_computation.4 | async-start | bytes 1572864 | tf_op jit(solution)/shard_map/all_gather | solution.py:129
  171.9 17.1 %collective-permute-start.4 = (bf16[16,2,4096]{2,0,1:T(8,128)(2,1)S(1)}, bf16[16,2,4096]{2,0,1:T(8,128)(2,1)S(1)}, u32[]{:S(2)}, u32[]{:S(2)}) collective-permute-start(bf16[16,2,4096]{2,0,1:T(8,128)(2,1)S(1)} %collective-permute-done.3), channel_id=1, source_target_pairs={{0,2},{2,4},{4,6},{6,8},{8,10},{10,12},{12,14},{14,0},{1,3},{3,5},... | collective-permute-start | bytes 786440 | tf_op jit(solution)/shard_map/ppermute | solution.py:141
  189.1 9.1 %collective-permute-start.5 = (bf16[16,2,4096]{2,0,1:T(8,128)(2,1)S(1)}, bf16[16,2,4096]{2,0,1:T(8,128)(2,1)S(1)}, u32[]{:S(2)}, u32[]{:S(2)}) collective-permute-start(bf16[16,2,4096]{2,0,1:T(8,128)(2,1)S(1)} %collective-permute-done.4), channel_id=1, source_target_pairs={{0,2},{2,4},{4,6},{6,8},{8,10},{10,12},{12,14},{14,0},{1,3},{3,5},... | collective-permute-start | bytes 786440 | tf_op jit(solution)/shard_map/ppermute | solution.py:141
  198.1 23.5 %collective-permute-start.6 = (bf16[16,2,4096]{2,0,1:T(8,128)(2,1)S(1)}, bf16[16,2,4096]{2,0,1:T(8,128)(2,1)S(1)}, u32[]{:S(2)}, u32[]{:S(2)}) collective-permute-start(bf16[16,2,4096]{2,0,1:T(8,128)(2,1)S(1)} %collective-permute-done.5), channel_id=1, source_target_pairs={{0,2},{2,4},{4,6},{6,8},{8,10},{10,12},{12,14},{14,0},{1,3},{3,5},... | collective-permute-start | bytes 786440 | tf_op jit(solution)/shard_map/ppermute | solution.py:141
  251.6 23.0 %copy-start.1 = (f32[4,2,2,2]{0,3,2,1:T(2,128)S(1)}, f32[4,2,2,2]{0,3,2,1:T(2,128)}, u32[]{:S(2)}) copy-start(f32[4,2,2,2]{0,3,2,1:T(2,128)} %param.10) | copy-start | bytes 388
Sparse Core Ops, SparseCore 0:
  221.7 10.3 all-gather.1
